TPU v7x, 32 devices: a whole 2x2x4 slice. The times are simulated.
32 devices in a mesh: seq: 16 (over z, y, x), bat: 2 (over core).
Axes of the slice: x: 2, y: 2, z: 4, core: 2. Of those that a mesh axis runs over, the one named last changes fastest.
Arguments:
- tokens: bfloat16 [2, 65536, 256], P('bat', 'seq'), may hold values from -6 to 6
- filter_spectrum: bfloat16 [2, 256, 256, 256], P(None, 'seq', None, 'bat'), may hold values from -6 to 6
- skip_gain: float32 [256], replicated, may hold values from 0.5 to 1.5
Outputs:
- mixed: bfloat16 [2, 65536, 256], P('bat', 'seq')
All inputs are finite; a program needn't handle non-finite values.
Results may differ from a plain program's by a relative error of at most 0.012.
Values may be sent and summed in bfloat16 or wider, within the bound.
A program may use at most 64 MiB of HBM per device.

v0:
```python
import math
import jax
import jax.numpy as jnp
from jax import lax
from jax.sharding import PartitionSpec as P

N1 = 256
N2 = 256


def cos_sin(points):
    steps_range = jnp.arange(points, dtype=jnp.int32)
    index_grid = steps_range[:, None] * steps_range[None, :] % points
    phase_angle = index_grid.astype(jnp.float32) * (2.0 * math.pi / points)
    return (jnp.cos(phase_angle), jnp.sin(phase_angle))


def real_table(points):
    cosine, sine_vals = cos_sin(points)
    return jnp.stack([cosine, -sine_vals], axis=1).astype(jnp.bfloat16)


def complex_table(points, signum, factor):
    cosine, sine_vals = cos_sin(points)
    top_rows = jnp.stack([cosine, signum * sine_vals], axis=1)
    low_rows = jnp.stack([-signum * sine_vals, cosine], axis=1)
    return (jnp.stack([top_rows, low_rows], axis=0) * factor).astype(jnp.bfloat16)


def final_table(points):
    cosine, sine_vals = cos_sin(points)
    return (jnp.stack([cosine, -sine_vals], axis=0) / points).astype(jnp.bfloat16)


def twiddle_phase(first_rows, second_rows, period):
    index_grid = first_rows[:, None] * second_rows[None, :] % period
    phase_angle = index_grid.astype(jnp.float32) * (2.0 * math.pi / period)
    return (jnp.cos(phase_angle)[..., None], jnp.sin(phase_angle)[..., None])


def multiply(values, filters):
    chosen = values.astype(jnp.float32)
    weights = lax.all_gather(filters, "bat", axis=3, tiled=True).astype(jnp.float32)[:, None]
    real_part = chosen[0] * weights[0] - chosen[1] * weights[1]
    imag_part = chosen[0] * weights[1] + chosen[1] * weights[0]
    return jnp.stack([real_part, imag_part]).astype(jnp.bfloat16)


def body(tokens, filter_spectrum, skip_gain):
    seq_count = lax.axis_size("seq")
    device_index = lax.axis_index("seq")
    batch_rows, local_length, channels = tokens.shape
    rows_local = N1 // seq_count
    cols_local = N2 // seq_count
    period = N1 * N2
    laid_out = tokens.reshape(batch_rows, rows_local, N2, channels)
    columns = lax.all_to_all(laid_out, "seq", split_axis=2, concat_axis=1, tiled=True)
    first_section = jnp.einsum(
        "bnmc,nsk->sbkmc", columns, real_table(N1), preferred_element_type=jnp.float32
    )
    own_cols = device_index * cols_local + jnp.arange(cols_local, dtype=jnp.int32)
    cos_tw, sin_tw = twiddle_phase(jnp.arange(N1, dtype=jnp.int32), own_cols, period)
    real_part = first_section[0] * cos_tw + first_section[1] * sin_tw
    imag_part = first_section[1] * cos_tw - first_section[0] * sin_tw
    turned = jnp.stack([real_part, imag_part]).astype(jnp.bfloat16)
    rows_block = lax.all_to_all(turned, "seq", split_axis=2, concat_axis=3, tiled=True)
    spectrum = jnp.einsum(
        "rbknc,rnsj->sbkjc",
        rows_block,
        complex_table(N2, -1.0, 1.0),
        preferred_element_type=jnp.float32,
    ).astype(jnp.bfloat16)
    product = multiply(spectrum, filter_spectrum)
    back_section = jnp.einsum(
        "rbkjc,rjsn->sbknc",
        product,
        complex_table(N2, 1.0, 1.0 / N2),
        preferred_element_type=jnp.float32,
    )
    own_rows = device_index * rows_local + jnp.arange(rows_local, dtype=jnp.int32)
    cos_back, sin_back = twiddle_phase(own_rows, jnp.arange(N2, dtype=jnp.int32), period)
    real_back = back_section[0] * cos_back - back_section[1] * sin_back
    imag_back = back_section[0] * sin_back + back_section[1] * cos_back
    turned_back = jnp.stack([real_back, imag_back]).astype(jnp.bfloat16)
    mixed_cols = lax.all_to_all(turned_back, "seq", split_axis=3, concat_axis=2, tiled=True)
    filtered = jnp.einsum(
        "rbknc,rkm->bmnc", mixed_cols, final_table(N1), preferred_element_type=jnp.float32
    )
    result = (filtered + skip_gain * columns.astype(jnp.float32)).astype(jnp.bfloat16)
    restored = lax.all_to_all(result, "seq", split_axis=1, concat_axis=2, tiled=True)
    return restored.reshape(batch_rows, local_length, channels)


def solution(mesh):
    placed = (P("bat", "seq", None), P(None, "seq", None, "bat"), P())
    return jax.shard_map(
        body, mesh=mesh, in_specs=placed, out_specs=P("bat", "seq", None), check_vma=False
    )
```

profile of v0, /device:TPU:0, one launch (start us, length us, event | category | flops | bytes accessed | tf_op | source)
XLA Modules:
  0.0 355.4 jit_solution(5459308199365572002)
XLA Ops:
  6.5 4.1 %copy.31 = bf16[1,16,256,256]{3,1,0,2:T(8,128)(2,1)} copy(bf16[1,16,256,256]{3,2,1,0:T(8,128)(2,1)} %bitcast.109) | data formatting | bytes 4194304 | tf_op jit(solution)/shard_map/reshape | solution.py:56
  10.6 8.3 %all-to-all-start = ((bf16[1,16,256,256]{3,1,0,2:T(8,128)(2,1)}), bf16[1,16,256,256]{3,1,0,2:T(8,128)(2,1)S(1)}, u32[]{:S(2)}, u32[]{:S(2)}) async-start(bf16[1,16,256,256]{3,1,0,2:T(8,128)(2,1)} %copy.31), calls=%async_computation | async-start | bytes 4194304 | tf_op jit(solution)/shard_map/all_to_all | solution.py:57
  20.2 41.8 %all-to-all-done = bf16[1,16,256,256]{3,1,0,2:T(8,128)(2,1)S(1)} async-done(((bf16[1,16,256,256]{3,1,0,2:T(8,128)(2,1)}), bf16[1,16,256,256]{3,1,0,2:T(8,128)(2,1)S(1)}, u32[]{:S(2)}, u32[]{:S(2)}) %all-to-all-start) | async-done | bytes 2097184 | tf_op jit(solution)/shard_map/all_to_all | solution.py:57
  62.7 1.2 copy.33
  63.9 1.3 fusion.18
  65.2 1.5 fusion.8
  67.0 4.3 %copy.34 = bf16[2,1,256,16,256]{4,3,1,0,2:T(8,128)(2,1)} copy(bf16[2,1,256,16,256]{4,2,3,1,0:T(8,128)(2,1)S(1)} %pad_maximum_fusion) | data formatting | bytes 8388608 | tf_op jit(solution)/shard_map/stack | solution.py:65
  71.3 10.1 %all-to-all-start.1 = ((bf16[2,1,256,16,256]{4,3,1,0,2:T(8,128)(2,1)}), bf16[2,1,256,16,256]{4,3,1,0,2:T(8,128)(2,1)}, u32[]{:S(2)}, u32[]{:S(2)}) async-start(bf16[2,1,256,16,256]{4,3,1,0,2:T(8,128)(2,1)} %copy.34), calls=%async_computation.1 | async-start | bytes 8388608 | tf_op jit(solution)/shard_map/all_to_all | solution.py:66
  86.2 11.6 %all-gather.2.cloned.1.call-done = bf16[2,16,256,256]{3,2,1,0:T(8,128)(2,1)} async-done(((bf16[2,16,256,128]{3,2,1,0:T(8,128)(2,1)}), bf16[2,16,256,256]{3,2,1,0:T(8,128)(2,1)}) %all-gather.2.cloned.1.call-update) | async-done | bytes 4194320 | tf_op jit(solution)/shard_map/all_gather | solution.py:43
  97.8 6.5 %convert_element_type.144 = f32[2,16,256,256]{3,2,1,0:T(8,128)} convert(bf16[2,16,256,256]{3,2,1,0:T(8,128)(2,1)} %all-gather.2.cloned.1.call-done) | non-fusion elementwise | flops 2097152 | bytes 12582912 | tf_op jit(solution)/shard_map/convert_element_type | solution.py:43
  104.3 55.5 %all-to-all-done.1 = bf16[2,1,256,16,256]{4,3,1,0,2:T(8,128)(2,1)} async-done(((bf16[2,1,256,16,256]{4,3,1,0,2:T(8,128)(2,1)}), bf16[2,1,256,16,256]{4,3,1,0,2:T(8,128)(2,1)}, u32[]{:S(2)}, u32[]{:S(2)}) %all-to-all-start.1) | async-done | bytes 4194336 | tf_op jit(solution)/shard_map/all_to_all | solution.py:66
  159.8 2.7 copy.35
  162.5 2.4 convert_bitcast_fusion.1
  166.0 1.8 subtract_convert_fusion.1
  167.8 2.4 fusion.5
  170.2 1.5 subtract_convert_fusion
  172.0 4.4 %copy.40 = bf16[2,1,16,256,256]{4,2,0,1,3:T(8,128)(2,1)} copy(bf16[2,1,16,256,256]{4,3,2,0,1:T(8,128)(2,1)S(1)} %pad_maximum_fusion.2) | data formatting | bytes 8388608 | tf_op jit(solution)/shard_map/stack | solution.py:84
  176.4 19.4 %all-to-all-start.2 = ((bf16[2,1,16,256,256]{4,2,0,1,3:T(8,128)(2,1)}), bf16[2,1,16,256,256]{4,2,0,1,3:T(8,128)(2,1)}, u32[]{:S(2)}, u32[]{:S(2)}) async-start(bf16[2,1,16,256,256]{4,2,0,1,3:T(8,128)(2,1)} %copy.40), calls=%async_computation.2 | async-start | bytes 8388608 | tf_op jit(solution)/shard_map/all_to_all | solution.py:85
  196.9 77.4 %all-to-all-done.2 = bf16[2,1,16,256,256]{4,2,0,1,3:T(8,128)(2,1)} async-done(((bf16[2,1,16,256,256]{4,2,0,1,3:T(8,128)(2,1)}), bf16[2,1,16,256,256]{4,2,0,1,3:T(8,128)(2,1)}, u32[]{:S(2)}, u32[]{:S(2)}) %all-to-all-start.2) | async-done | bytes 4194336 | tf_op jit(solution)/shard_map/all_to_all | solution.py:85
  274.3 2.7 copy.41
  277.0 1.3 fusion.10
  278.4 1.2 copy.42
  279.6 67.4 %all_to_all.60 = bf16[1,256,16,256]{3,2,0,1:T(8,128)(2,1)S(1)} all-to-all(bf16[1,256,16,256]{3,2,0,1:T(8,128)(2,1)S(1)} %copy.42), channel_id=1, replica_groups=mesh['seq'=16,'bat'=2] {'seq'}, dimensions={1} | all-to-all | bytes 4194304 | tf_op jit(solution)/shard_map/all_to_all | solution.py:90
  347.0 1.5 copy.43
  (24 shorter events, 9.6 us)
Async XLA Ops:
  10.6 51.4 %all-to-all-start = ((bf16[1,16,256,256]{3,1,0,2:T(8,128)(2,1)}), bf16[1,16,256,256]{3,1,0,2:T(8,128)(2,1)S(1)}, u32[]{:S(2)}, u32[]{:S(2)}) async-start(bf16[1,16,256,256]{3,1,0,2:T(8,128)(2,1)} %copy.31), calls=%async_computation | async-start | bytes 4194304 | tf_op jit(solution)/shard_map/all_to_all | solution.py:57
  71.3 88.5 %all-to-all-start.1 = ((bf16[2,1,256,16,256]{4,3,1,0,2:T(8,128)(2,1)}), bf16[2,1,256,16,256]{4,3,1,0,2:T(8,128)(2,1)}, u32[]{:S(2)}, u32[]{:S(2)}) async-start(bf16[2,1,256,16,256]{4,3,1,0,2:T(8,128)(2,1)} %copy.34), calls=%async_computation.1 | async-start | bytes 8388608 | tf_op jit(solution)/shard_map/all_to_all | solution.py:66
  81.4 16.4 %all-gather.2.cloned.1.call-start = ((), (), s32[]{:S(2)}) async-start(), calls=%async_computation.4 | async-start | bytes 6291456 | tf_op jit(solution)/shard_map/all_gather | solution.py:43
  162.5 2.4 slice-start
  162.5 3.5 slice-start.1
  166.0 1.8 copy-start
  176.4 97.9 %all-to-all-start.2 = ((bf16[2,1,16,256,256]{4,2,0,1,3:T(8,128)(2,1)}), bf16[2,1,16,256,256]{4,2,0,1,3:T(8,128)(2,1)}, u32[]{:S(2)}, u32[]{:S(2)}) async-start(bf16[2,1,16,256,256]{4,2,0,1,3:T(8,128)(2,1)} %copy.40), calls=%async_computation.2 | async-start | bytes 8388608 | tf_op jit(solution)/shard_map/all_to_all | solution.py:85
  274.3 2.8 copy-start.1
Sparse Core Ops, SparseCore 0:
  83.7 13.9 all-gather.1
where the time goes:
time: 356 us; the launch traced here: 355 us
  waiting for transfers between devices  187 us (53%)
  blocking collectives  67.4 us (19%)
  starting transfers between devices  38 us (11%)
  local copies, waits for them, and re-layouts  24 us (7%)
  other arithmetic  18.3 us (5%)
  between operations  13.6 us (4%)
  matrix products  7.29 us (2%)
    all_to_all x1, waiting for transfers between devices, body(): lax.all_to_all(turned_back, 'seq', split_axis=3, concat_axis=2, tiled=True)  77.4 us
    all_to_all x1, blocking collectives, body(): lax.all_to_all(result, 'seq', split_axis=1, concat_axis=2, tiled=True)  67.4 us
    all_to_all x1, waiting for transfers between devices, body(): lax.all_to_all(turned, 'seq', split_axis=2, concat_axis=3, tiled=True)  55.5 us
    all_to_all x1, waiting for transfers between devices, body(): lax.all_to_all(laid_out, 'seq', split_axis=2, concat_axis=1, tiled=True)  41.8 us
    all_to_all x1, starting transfers between devices, body(): lax.all_to_all(turned_back, 'seq', split_axis=3, concat_axis=2, tiled=True)  19.4 us
    all_gather x1, waiting for transfers between devices, multiply(): lax.all_gather(filters, 'bat', axis=3, tiled=True).astype(jnp.float32)  11.6 us
    all_to_all x1, starting transfers between devices, body(): lax.all_to_all(turned, 'seq', split_axis=2, concat_axis=3, tiled=True)  10.1 us
    all_to_all x1, starting transfers between devices, body(): lax.all_to_all(laid_out, 'seq', split_axis=2, concat_axis=1, tiled=True)  8.34 us
  transfers between devices with their start and end apart: 4, of which 4 were waited for; matrix products, arithmetic and copies ran while one was open for 4% of the time, Pallas kernels for 0%

commit v1 on v0

--- a/solution.py
+++ b/solution.py
@@ -1,11 +1,28 @@
+import functools
 import math
 import jax
 import jax.numpy as jnp
 from jax import lax
 from jax.sharding import PartitionSpec as P
+from jax.lax import all_to_all, axis_size
 
 N1 = 256
 N2 = 256
+
+
+def pass_axis_part(q_in, mesh_ax):
+    return jnp.concatenate(
+        all_to_all(
+            jnp.stack(jnp.split(q_in, axis_size(mesh_ax), 2)),
+            concat_axis=0,
+            split_axis=0,
+            axis_name=mesh_ax,
+        ),
+        3,
+    )
+
+
+vectors_fix = functools.partial(pass_axis_part, mesh_ax="seq")
 
 
 def cos_sin(points):
@@ -63,7 +80,7 @@
     real_part = first_section[0] * cos_tw + first_section[1] * sin_tw
     imag_part = first_section[1] * cos_tw - first_section[0] * sin_tw
     turned = jnp.stack([real_part, imag_part]).astype(jnp.bfloat16)
-    rows_block = lax.all_to_all(turned, "seq", split_axis=2, concat_axis=3, tiled=True)
+    rows_block = vectors_fix(turned)
     spectrum = jnp.einsum(
         "rbknc,rnsj->sbkjc",
         rows_block,

time: 356 us -> 370 us (1.039)
  local copies, waits for them, and re-layouts: 24 us -> 32.3 us
  matrix products: 7.29 us -> 11.4 us
    unnamed x8 -> x21, local copies, waits for them, and re-layouts: 1.09 us -> 10.8 us
    reshape x0 -> x1, local copies, waits for them, and re-layouts: none -> 5.65 us  [pass_axis_part(): jnp.concatenate(all_to_all(jnp.stack(jnp.split(q_in, axis_size(mesh_ax),...]
    another operation x1 -> x0, local copies, waits for them, and re-layouts: 4.31 us -> none  [body(): turned = jnp.stack([real_part, imag_part]).astype(jnp.bfloat16)]
  transfers between devices with their start and end apart: 4 -> 4, of which waited for: 4 -> 4; matrix products, arithmetic and copies ran while one was open for 4% -> 3% of each run, Pallas kernels for 0% -> 0%
where the time goes in v1:
time: 370 us
  waiting for transfers between devices  187 us (51%)
  blocking collectives  67.5 us (18%)
  starting transfers between devices  38 us (10%)
  local copies, waits for them, and re-layouts  32.3 us (9%)
  other arithmetic  20.2 us (5%)
  between operations  13.6 us (4%)
  matrix products  11.4 us (3%)
    all_to_all x1, waiting for transfers between devices, body(): lax.all_to_all(turned_back, 'seq', split_axis=3, concat_axis=2, tiled=True)  77.4 us
    all_to_all x1, blocking collectives, body(): lax.all_to_all(result, 'seq', split_axis=1, concat_axis=2, tiled=True)  67.5 us
    all_to_all x1, waiting for transfers between devices, pass_axis_part(): all_to_all(jnp.stack(jnp.split(q_in, axis_size(mesh_ax), 2)), concat_axis...  55.5 us
    all_to_all x1, waiting for transfers between devices, body(): lax.all_to_all(laid_out, 'seq', split_axis=2, concat_axis=1, tiled=True)  41.8 us
    all_to_all x1, starting transfers between devices, body(): lax.all_to_all(turned_back, 'seq', split_axis=3, concat_axis=2, tiled=True)  19.4 us
    all_gather x1, waiting for transfers between devices, multiply(): lax.all_gather(filters, 'bat', axis=3, tiled=True).astype(jnp.float32)  11.6 us
    unnamed x21, local copies, waits for them, and re-layouts  10.8 us
    all_to_all x1, starting transfers between devices, pass_axis_part(): all_to_all(jnp.stack(jnp.split(q_in, axis_size(mesh_ax), 2)), concat_axis...  10.1 us
  transfers between devices with their start and end apart: 4, of which 4 were waited for; matrix products, arithmetic and copies ran while one was open for 3% of the time, Pallas kernels for 0%

profile of v1, /device:TPU:0, one launch (start us, length us, event | category | flops | bytes accessed | tf_op | source)
XLA Modules:
  0.0 369.7 jit_solution(15648905718847209327)
XLA Ops:
  6.5 4.1 %copy.76 = bf16[1,16,256,256]{3,1,0,2:T(8,128)(2,1)} copy(bf16[1,16,256,256]{3,2,1,0:T(8,128)(2,1)} %bitcast.189) | data formatting | bytes 4194304 | tf_op jit(solution)/shard_map/reshape | solution.py:73
  10.6 8.3 %all-to-all-start = ((bf16[1,16,256,256]{3,1,0,2:T(8,128)(2,1)}), bf16[1,16,256,256]{3,1,0,2:T(8,128)(2,1)S(1)}, u32[]{:S(2)}, u32[]{:S(2)}) async-start(bf16[1,16,256,256]{3,1,0,2:T(8,128)(2,1)} %copy.76), calls=%async_computation | async-start | bytes 4194304 | tf_op jit(solution)/shard_map/all_to_all | solution.py:74
  19.0 1.1 negate_convert_fusion
  20.2 41.8 %all-to-all-done = bf16[1,16,256,256]{3,1,0,2:T(8,128)(2,1)S(1)} async-done(((bf16[1,16,256,256]{3,1,0,2:T(8,128)(2,1)}), bf16[1,16,256,256]{3,1,0,2:T(8,128)(2,1)S(1)}, u32[]{:S(2)}, u32[]{:S(2)}) %all-to-all-start) | async-done | bytes 2097184 | tf_op jit(solution)/shard_map/all_to_all | solution.py:74
  62.7 1.2 copy.78
  63.9 1.3 fusion.25
  65.2 1.5 fusion.14
  78.5 10.1 %all-to-all-start.1 = ((bf16[16,2,1,16,16,256]{5,3,4,1,2,0:T(8,128)(2,1)}), bf16[16,2,1,16,16,256]{5,3,4,1,2,0:T(8,128)(2,1)}, u32[]{:S(2)}, u32[]{:S(2)}) async-start(bf16[16,2,1,16,16,256]{5,3,4,1,2,0:T(8,128)(2,1)} %bitcast_dynamic-update-slice_fusion), calls=%async_computation.1 | async-start | bytes 8388608 | tf_op jit(solution)/shard_map/all_to_all | solution.py:15
  93.4 11.6 %all-gather.2.cloned.1.call-done = bf16[2,16,256,256]{3,2,1,0:T(8,128)(2,1)} async-done(((bf16[2,16,256,128]{3,2,1,0:T(8,128)(2,1)}), bf16[2,16,256,256]{3,2,1,0:T(8,128)(2,1)}) %all-gather.2.cloned.1.call-update) | async-done | bytes 4194320 | tf_op jit(solution)/shard_map/all_gather | solution.py:60
  105.0 6.5 %convert_element_type.144 = f32[2,16,256,256]{3,2,1,0:T(8,128)} convert(bf16[2,16,256,256]{3,2,1,0:T(8,128)(2,1)} %all-gather.2.cloned.1.call-done) | non-fusion elementwise | flops 2097152 | bytes 12582912 | tf_op jit(solution)/shard_map/convert_element_type | solution.py:60
  111.5 55.5 %all-to-all-done.1 = bf16[16,2,1,16,16,256]{5,3,4,1,2,0:T(8,128)(2,1)} async-done(((bf16[16,2,1,16,16,256]{5,3,4,1,2,0:T(8,128)(2,1)}), bf16[16,2,1,16,16,256]{5,3,4,1,2,0:T(8,128)(2,1)}, u32[]{:S(2)}, u32[]{:S(2)}) %all-to-all-start.1) | async-done | bytes 4194336 | tf_op jit(solution)/shard_map/all_to_all | solution.py:15
  167.0 5.7 %copy.94 = bf16[2,1,16,16,16,256]{5,4,3,2,0,1:T(8,128)(2,1)} copy(bf16[2,1,16,16,16,256]{5,2,4,0,1,3:T(8,128)(2,1)} %bitcast.47) | data formatting | bytes 8388608 | tf_op jit(solution)/shard_map/reshape | solution.py:14
  172.6 4.7 %convert_bitcast_fusion.1 = (f32[2,1,16,256,256]{4,3,2,0,1:T(8,128)S(1)}, f32[2,1,16,256,256]{4,3,2,1,0:T(8,128)S(1)}) fusion(bf16[2,16,256,256]{3,2,1,0:T(8,128)(2,1)} %bitcast.186, bf16[1,256,2,256]{1,3,2,0:T(8,128)(2,1)S(1)} %get-tuple-element.16, bf16[1,256,2,256]{1,3,2,0:T(8,128)(2,1)S(1)} %get-tuple-element.15), kind=kOutput, calls=%fused_computation.1 | convolution fusion | flops 2151940096 | bytes 21495808 | tf_op jit(solution)/shard_map/rbknc,rnsj->sbkjc/dot_general | solution.py:84
  177.4 2.9 subtract_convert_fusion.1
  180.3 4.1 %fusion.9 = f32[2,1,16,256,256]{4,3,2,0,1:T(8,128)S(1)} fusion(bf16[1,16,256,256]{3,2,1,0:T(8,128)(2,1)} %get-tuple-element.6, bf16[1,16,256,256]{3,2,1,0:T(8,128)(2,1)S(1)} %get-tuple-element.5, f32[1,256,2,256]{1,3,2,0:T(8,128)} %get-tuple-element.14, f32[1,256,2,256]{1,3,2,0:T(8,128)S(1)} %get-tuple-element.13), kind=kOutput, calls=%fused_computation.26 | convolution fusion | flops 2150367232 | bytes 13631488 | tf_op jit(solution)/shard_map/rbkjc,rjsn->sbknc/dot_general | solution.py:91
  184.4 1.5 subtract_convert_fusion
  186.3 4.4 %copy.100 = bf16[2,1,16,256,256]{4,2,0,1,3:T(8,128)(2,1)} copy(bf16[2,1,16,256,256]{4,3,2,0,1:T(8,128)(2,1)S(1)} %pad_maximum_fusion.2) | data formatting | bytes 8388608 | tf_op jit(solution)/shard_map/stack | solution.py:101
  190.7 19.4 %all-to-all-start.2 = ((bf16[2,1,16,256,256]{4,2,0,1,3:T(8,128)(2,1)}), bf16[2,1,16,256,256]{4,2,0,1,3:T(8,128)(2,1)}, u32[]{:S(2)}, u32[]{:S(2)}) async-start(bf16[2,1,16,256,256]{4,2,0,1,3:T(8,128)(2,1)} %copy.100), calls=%async_computation.2 | async-start | bytes 8388608 | tf_op jit(solution)/shard_map/all_to_all | solution.py:102
  211.1 77.4 %all-to-all-done.2 = bf16[2,1,16,256,256]{4,2,0,1,3:T(8,128)(2,1)} async-done(((bf16[2,1,16,256,256]{4,2,0,1,3:T(8,128)(2,1)}), bf16[2,1,16,256,256]{4,2,0,1,3:T(8,128)(2,1)}, u32[]{:S(2)}, u32[]{:S(2)}) %all-to-all-start.2) | async-done | bytes 4194336 | tf_op jit(solution)/shard_map/all_to_all | solution.py:102
  288.5 2.7 copy.101
  291.3 1.3 fusion.16
  292.6 1.2 copy.102
  293.8 67.5 %all_to_all.50 = bf16[1,256,16,256]{3,2,0,1:T(8,128)(2,1)S(1)} all-to-all(bf16[1,256,16,256]{3,2,0,1:T(8,128)(2,1)S(1)} %copy.102), channel_id=1, replica_groups=mesh['seq'=16,'bat'=2] {'seq'}, dimensions={1} | all-to-all | bytes 4194304 | tf_op jit(solution)/shard_map/all_to_all | solution.py:107
  361.3 1.5 copy.103
  (37 shorter events, 19.0 us)
Async XLA Ops:
  10.6 51.4 %all-to-all-start = ((bf16[1,16,256,256]{3,1,0,2:T(8,128)(2,1)}), bf16[1,16,256,256]{3,1,0,2:T(8,128)(2,1)S(1)}, u32[]{:S(2)}, u32[]{:S(2)}) async-start(bf16[1,16,256,256]{3,1,0,2:T(8,128)(2,1)} %copy.76), calls=%async_computation | async-start | bytes 4194304 | tf_op jit(solution)/shard_map/all_to_all | solution.py:74
  78.5 88.5 %all-to-all-start.1 = ((bf16[16,2,1,16,16,256]{5,3,4,1,2,0:T(8,128)(2,1)}), bf16[16,2,1,16,16,256]{5,3,4,1,2,0:T(8,128)(2,1)}, u32[]{:S(2)}, u32[]{:S(2)}) async-start(bf16[16,2,1,16,16,256]{5,3,4,1,2,0:T(8,128)(2,1)} %bitcast_dynamic-update-slice_fusion), calls=%async_computation.1 | async-start | bytes 8388608 | tf_op jit(solution)/shard_map/all_to_all | solution.py:15
  88.6 16.4 %all-gather.2.cloned.1.call-start = ((), (), s32[]{:S(2)}) async-start(), calls=%async_computation.4 | async-start | bytes 6291456 | tf_op jit(solution)/shard_map/all_gather | solution.py:60
  172.6 4.7 %slice-start = ((s8[8388608]{0:T(1024)(128)(4,1)}), s8[4194304]{0:T(1024)(128)(4,1)S(1)}, s32[]{:S(2)}) async-start(s8[8388608]{0:T(1024)(128)(4,1)} %bitcast.181), calls=%async_computation.5 | async-start | bytes 8388608
  172.6 4.7 %slice-start.1 = ((s8[8388608]{0:T(1024)(128)(4,1)}), s8[4194304]{0:T(1024)(128)(4,1)S(1)}, s32[]{:S(2)}) async-start(s8[8388608]{0:T(1024)(128)(4,1)} %bitcast.181), calls=%async_computation.6 | async-start | bytes 8388608
  190.7 97.9 %all-to-all-start.2 = ((bf16[2,1,16,256,256]{4,2,0,1,3:T(8,128)(2,1)}), bf16[2,1,16,256,256]{4,2,0,1,3:T(8,128)(2,1)}, u32[]{:S(2)}, u32[]{:S(2)}) async-start(bf16[2,1,16,256,256]{4,2,0,1,3:T(8,128)(2,1)} %copy.100), calls=%async_computation.2 | async-start | bytes 8388608 | tf_op jit(solution)/shard_map/all_to_all | solution.py:102
  288.5 2.8 copy-start
Sparse Core Ops, SparseCore 0:
  90.9 13.9 all-gather.1
